TPU v7x, 16 devices: a 4x2x1 block of a 4x4x8 slice. The times are simulated.
16 devices in a mesh: dp: 2 (over y, z), tp: 8 (over x, core).
Axes of the slice: x: 4, y: 2, z: 1, core: 2. Of those that a mesh axis runs over, the one named last changes fastest.
The devices are a block of a 4x4x8 slice.
Arguments:
- act_in: bfloat16 [512, 5120], P('dp'), parts along dimension 0
- w_qkv: bfloat16 [2, 5120, 40, 3, 128], P(None, None, 'tp')
- w_out: bfloat16 [2, 40, 128, 5120], P(None, 'tp')
- w_up: bfloat16 [2, 5120, 20480], P(None, None, 'tp')
- w_down: bfloat16 [2, 20480, 5120], P(None, 'tp')
- gain_one: float32 [2, 5120], replicated
- gain_two: float32 [2, 5120], replicated
Outputs:
- output: bfloat16 [512, 5120], P('dp'), parts along dimension 0
There are 2 independent parts. A program takes and returns all parts, laid end to end along the dimension named above; an argument that names none is the same for every part.
All inputs are finite; a program needn't handle non-finite values.
Results may differ from a plain program's by a relative error of at most 0.0165387.
Values are sent between devices in bfloat16 or wider.
A program may use at most 768 MiB of HBM per device.

v0:
```python
import math
import jax
import jax.numpy as jnp
from jax import lax
from jax.sharding import PartitionSpec as P


def layer_norm(act_rows, gain_vec):
    rows_f32 = act_rows.astype(jnp.float32)
    centred = rows_f32 - jnp.mean(rows_f32, axis=-1, keepdims=True)
    var_rows = jnp.mean(centred * centred, axis=-1, keepdims=True)
    return (centred * lax.rsqrt(var_rows + 1e-5) * gain_vec).astype(jnp.bfloat16)


def causal_attention(query_rows, key_rows, value_rows, query_start):
    n_q, num_heads, head_dim = query_rows.shape
    seq_k = key_rows.shape[0]
    limit_rows = max(8, 2 ** 24 // (num_heads * seq_k))
    row_block = math.gcd(n_q, 2 ** int(math.log2(limit_rows)))
    score_scale = 1.0 / math.sqrt(head_dim)
    key_pos = jnp.arange(seq_k)

    def one_block(blk_idx):
        row_start = blk_idx * row_block
        q_blk = lax.dynamic_slice_in_dim(query_rows, row_start, row_block, axis=0)
        scores = jnp.einsum("qhd,khd->hqk", q_blk, key_rows, preferred_element_type=jnp.float32) * score_scale
        q_pos = query_start + row_start + jnp.arange(row_block)
        scores = jnp.where(key_pos[None, None, :] <= q_pos[None, :, None], scores, -1e30)
        exp_scores = jnp.exp(scores - jnp.max(scores, axis=-1, keepdims=True))
        prob_sum = jnp.sum(exp_scores, axis=-1)
        mix_out = jnp.einsum("hqk,khd->qhd", exp_scores.astype(jnp.bfloat16), value_rows, preferred_element_type=jnp.float32)
        return (mix_out / prob_sum.T[:, :, None]).astype(jnp.bfloat16)

    blocks = lax.map(one_block, jnp.arange(n_q // row_block))
    return blocks.reshape(n_q, num_heads, head_dim)


def solution(mesh):
    def device_fn(act_in, w_qkv, w_out, w_up, w_down, gain_one, gain_two):
        act_rows = act_in
        for layer_idx in range(w_qkv.shape[0]):
            normed = layer_norm(act_rows, gain_one[layer_idx])
            qkv_rows = jnp.einsum("sm,mhcd->shcd", normed, w_qkv[layer_idx], preferred_element_type=jnp.float32).astype(jnp.bfloat16)
            attn_rows = causal_attention(qkv_rows[:, :, 0], qkv_rows[:, :, 1], qkv_rows[:, :, 2], 0)
            part_sum = jnp.einsum("shd,hdm->sm", attn_rows, w_out[layer_idx], preferred_element_type=jnp.float32).astype(jnp.bfloat16)
            attn_sum = lax.psum(part_sum, "tp")
            act_rows = (act_rows.astype(jnp.float32) + attn_sum.astype(jnp.float32)).astype(jnp.bfloat16)
            normed = layer_norm(act_rows, gain_two[layer_idx])
            hidden = jax.nn.gelu(jnp.dot(normed, w_up[layer_idx], preferred_element_type=jnp.float32), approximate=True).astype(jnp.bfloat16)
            part_sum = jnp.dot(hidden, w_down[layer_idx], preferred_element_type=jnp.float32).astype(jnp.bfloat16)
            mlp_sum = lax.psum(part_sum, "tp")
            act_rows = (act_rows.astype(jnp.float32) + mlp_sum.astype(jnp.float32)).astype(jnp.bfloat16)
        return act_rows

    return jax.shard_map(
        device_fn,
        mesh=mesh,
        in_specs=(
            P("dp", None),
            P(None, None, "tp", None, None),
            P(None, "tp", None, None),
            P(None, None, "tp"),
            P(None, "tp", None),
            P(None, None),
            P(None, None),
        ),
        out_specs=P("dp", None),
        check_vma=False,
    )
```

profile of v0, /device:TPU:113, one launch (start us, length us, event | category | flops | bytes accessed | tf_op | source)
XLA Modules:
  0.0 361.8 jit_solution(8306358509216900281)
XLA Ops:
  6.6 2.3 convert_reduce_fusion.3
  8.9 0.1 copy-done
  9.1 0.8 fusion.51
  10.0 12.2 %fusion.110 = bf16[256,5,3,128]{3,0,2,1:T(8,128)(2,1)S(1)} fusion(bf16[2,5120,5,3,128]{4,1,3,2,0:T(8,128)(2,1)} %param.8, bf16[256,5120]{1,0:T(8,128)(2,1)S(1)} %copy-done, f32[5120]{0:T(1024)S(1)} %bitcast.123, f32[256]{0:T(256)S(1)} %add_rsqrt_fusion.3, f32[256]{0:T(256)S(1)} %broadcast_multiply_fusion.3), kind=kOutput, calls=%fused_computation.96 | convolution fusion | flops 5040209920 | bytes 23287808 | tf_op jit(solution)/shard_map/sm,mhcd->shcd/dot_general | solution.py:43
  22.2 0.4 fusion.161
  22.6 1.1 copy-done.5
  23.6 0.2 fusion.134
  23.8 6.5 %fusion.28 = bf16[256,5120]{1,0:T(8,128)(2,1)} fusion(bf16[2,5,128,5120]{3,2,1,0:T(8,128)(2,1)} %param.9, f32[5,256,256]{1,2,0:T(8,128)} %copy-done.5, f32[5,256]{1,0:T(8,128)S(1)} %get-tuple-element.50, bf16[256,5,3,128]{3,0,2,1:T(8,128)(2,1)} %copy-done.9, f32[256,5]{0,1:T(8,128)S(1)} %bitcast.124), kind=kOutput, calls=%fused_computation.38 | convolution fusion | flops 1763901440 | bytes 10823680 | tf_op jit(solution)/shard_map/shd,hdm->sm/dot_general | solution.py:45
  30.4 0.2 all-reduce.7.cloned.1.call-start
  30.6 0.5 copy-done.7
  31.1 59.5 %all-reduce.5.cloned.1.call-done = bf16[256,5120]{1,0:T(8,128)(2,1)} async-done(((bf16[256,5120]{1,0:T(8,128)(2,1)}), bf16[256,5120]{1,0:T(8,128)(2,1)}) %all-reduce.5.cloned.1.call-update) | async-done | bytes 2621456 | tf_op jit(solution)/shard_map/psum | solution.py:46
  90.7 2.8 convert_reduce_fusion.2
  93.4 1.5 copy-done.1
  94.9 0.8 fusion.48
  95.8 24.4 %fusion.22 = bf16[256,5120]{1,0:T(8,128)(2,1)} fusion(bf16[2,2560,5120]{2,1,0:T(8,128)(2,1)} %param.11, bf16[2,5120,2560]{2,1,0:T(8,128)(2,1)} %param.10, bf16[256,5120]{1,0:T(8,128)(2,1)} %copy-done.1, f32[5120]{0:T(1024)S(1)} %bitcast.122, f32[256]{0:T(256)S(1)} %add_rsqrt_fusion.2, f32[256]{0:T(256)S(1)} %broadcast_multiply_fusion.2), kind=kOutput, calls=%fused_computation.36 | convolution fusion | flops 13435535360 | bytes 57694208 | tf_op jit(solution)/shard_map/dot_general | solution.py:50
  120.2 0.3 all-reduce.9.cloned.1.call-start
  120.5 58.5 %all-reduce.7.cloned.1.call-done = bf16[256,5120]{1,0:T(8,128)(2,1)} async-done(((bf16[256,5120]{1,0:T(8,128)(2,1)}), bf16[256,5120]{1,0:T(8,128)(2,1)}) %all-reduce.7.cloned.1.call-update) | async-done | bytes 2621456 | tf_op jit(solution)/shard_map/psum | solution.py:51
  179.1 3.6 convert_reduce_fusion.1
  182.6 0.8 fusion.45
  183.5 12.2 %fusion.115 = bf16[256,5,3,128]{3,0,2,1:T(8,128)(2,1)S(1)} fusion(bf16[2,5120,5,3,128]{4,1,3,2,0:T(8,128)(2,1)} %param.8, bf16[256,5120]{1,0:T(8,128)(2,1)S(1)} %get-tuple-element.36, f32[5120]{0:T(1024)S(1)} %bitcast.121, f32[256]{0:T(256)S(1)} %add_rsqrt_fusion.1, f32[256]{0:T(256)S(1)} %broadcast_multiply_fusion.1), kind=kOutput, calls=%fused_computation.97 | convolution fusion | flops 5040209920 | bytes 23287808 | tf_op jit(solution)/shard_map/sm,mhcd->shcd/dot_general | solution.py:43
  195.7 0.4 fusion.162
  196.1 1.1 copy-done.4
  197.2 0.2 fusion.136
  197.4 6.5 %fusion.31 = bf16[256,5120]{1,0:T(8,128)(2,1)} fusion(bf16[2,5,128,5120]{3,2,1,0:T(8,128)(2,1)} %param.9, f32[5,256,256]{1,2,0:T(8,128)} %copy-done.4, f32[5,256]{1,0:T(8,128)S(1)} %get-tuple-element.53, bf16[256,5,3,128]{3,0,2,1:T(8,128)(2,1)} %copy-done.8, f32[256,5]{0,1:T(8,128)S(1)} %bitcast.125), kind=kOutput, calls=%fused_computation.39 | convolution fusion | flops 1763901440 | bytes 10823680 | tf_op jit(solution)/shard_map/shd,hdm->sm/dot_general | solution.py:45
  203.9 0.3 all-reduce.11.cloned.1.call-start
  204.2 58.5 %all-reduce.9.cloned.1.call-done = bf16[256,5120]{1,0:T(8,128)(2,1)} async-done(((bf16[256,5120]{1,0:T(8,128)(2,1)}), bf16[256,5120]{1,0:T(8,128)(2,1)}) %all-reduce.9.cloned.1.call-update) | async-done | bytes 2621456 | tf_op jit(solution)/shard_map/psum | solution.py:46
  262.7 2.8 convert_reduce_fusion
  265.5 1.5 copy-done.2
  267.0 0.8 fusion.42
  267.8 24.3 %fusion.25 = bf16[256,5120]{1,0:T(8,128)(2,1)} fusion(bf16[2,2560,5120]{2,1,0:T(8,128)(2,1)} %param.11, bf16[2,5120,2560]{2,1,0:T(8,128)(2,1)} %param.10, bf16[256,5120]{1,0:T(8,128)(2,1)} %copy-done.2, f32[5120]{0:T(1024)S(1)} %bitcast.120, f32[256]{0:T(256)S(1)} %add_rsqrt_fusion, f32[256]{0:T(256)S(1)} %broadcast_multiply_fusion), kind=kOutput, calls=%fused_computation.37 | convolution fusion | flops 13435535360 | bytes 57694208 | tf_op jit(solution)/shard_map/dot_general | solution.py:50
  292.2 58.8 %all-reduce.11.cloned.1.call-done = bf16[256,5120]{1,0:T(8,128)(2,1)} async-done(((bf16[256,5120]{1,0:T(8,128)(2,1)}), bf16[256,5120]{1,0:T(8,128)(2,1)}) %all-reduce.11.cloned.1.call-update) | async-done | bytes 2621456 | tf_op jit(solution)/shard_map/psum | solution.py:51
  351.1 4.2 %fusion.57 = bf16[256,5120]{1,0:T(8,128)(2,1)} fusion(bf16[256,5120]{1,0:T(8,128)(2,1)S(1)} %copy-done.3, bf16[256,5120]{1,0:T(8,128)(2,1)} %all-reduce.11.cloned.1.call-done), kind=kLoop, calls=%fused_computation.63 | loop fusion | flops 5242880 | bytes 7864320 | tf_op jit(solution)/shard_map/convert_element_type | solution.py:52
  (30 shorter events, 0.4 us)
Async XLA Ops:
  6.5 2.5 copy-start
  6.5 84.1 %all-reduce.5.cloned.1.call-start = ((), (), s32[]{:S(2)}) async-start(), calls=%async_computation | async-start | bytes 5242880 | tf_op jit(solution)/shard_map/psum | solution.py:46
  6.6 3.3 copy-start.6
  22.2 1.6 copy-start.9
  22.6 1.1 copy-start.5
  30.3 0.8 copy-start.7
  30.4 148.7 %all-reduce.7.cloned.1.call-start = ((), (), s32[]{:S(2)}) async-start(), calls=%async_computation.1 | async-start | bytes 5242880 | tf_op jit(solution)/shard_map/psum | solution.py:51
  93.4 1.5 copy-start.1
  120.2 142.5 %all-reduce.9.cloned.1.call-start = ((), (), s32[]{:S(2)}) async-start(), calls=%async_computation.2 | async-start | bytes 5242880 | tf_op jit(solution)/shard_map/psum | solution.py:46
  195.7 1.6 copy-start.8
  196.1 1.1 copy-start.4
  203.9 147.2 %all-reduce.11.cloned.1.call-start = ((), (), s32[]{:S(2)}) async-start(), calls=%async_computation.3 | async-start | bytes 5242880 | tf_op jit(solution)/shard_map/psum | solution.py:51
  265.5 1.5 copy-start.2
  292.2 58.9 %copy-start.3 = (bf16[256,5120]{1,0:T(8,128)(2,1)S(1)}, bf16[256,5120]{1,0:T(8,128)(2,1)}, u32[]{:S(2)}) copy-start(bf16[256,5120]{1,0:T(8,128)(2,1)} %copy-done.2) | copy-start | bytes 7864324
Sparse Core Ops, SparseCore 0:
  30.5 60.1 all-reduce.4
  120.4 58.6 all-reduce.6
  204.0 58.6 all-reduce.8
  292.3 58.6 all-reduce.10
where the time goes:
time: 364 us; the launch traced here: 362 us
  waiting for transfers between devices  236 us (65%)
  matrix products  86.8 us (24%)
  other arithmetic  19.4 us (5%)
  between operations  13.3 us (4%)
  local copies, waits for them, and re-layouts  5.76 us (2%)
    psum x2, waiting for transfers between devices, device_fn(): attn_sum = lax.psum(part_sum, 'tp')  118 us
    psum x2, waiting for transfers between devices, device_fn(): mlp_sum = lax.psum(part_sum, 'tp')  117 us
    dot_general x2, matrix products, device_fn(): jnp.dot(hidden, w_down[layer_idx], preferred_element_type=jnp.float32)  48.7 us
    dot_general x2, matrix products, device_fn(): jnp.einsum('sm,mhcd->shcd', normed, w_qkv[layer_idx], preferred_element_t...  24.5 us
    dot_general x2, matrix products, device_fn(): jnp.einsum('shd,hdm->sm', attn_rows, w_out[layer_idx], preferred_element_...  12.9 us
    reduce_sum x4, other arithmetic, layer_norm(): centred = rows_f32 - jnp.mean(rows_f32, axis=-1, keepdims=True)  11.4 us
  transfers between devices with their start and end apart: 4, of which 4 were waited for; matrix products, arithmetic and copies ran while one was open for 0% of the time, Pallas kernels for 0%

commit v1 on v0

v1 whole, which is shorter than its diff:
```python
import functools
import math

import jax
import jax.numpy as jnp
from jax import lax
from jax.experimental import pallas as pl
from jax.experimental.pallas import tpu as pltpu
from jax.sharding import PartitionSpec as P

F32 = jnp.float32
BF16 = jnp.bfloat16
SLOTS = 12
LOADS = 24
PAIR, M1R, M1L, M2R, M2L, M3R, M3L = 0, 4, 5, 6, 7, 8, 9
STAT = 10
OWN_RA, OWN_RB, OWN_LA, OWN_LB, FWD_R, FWD_L = 18, 19, 20, 21, 22, 23
SH_OWN, SH_LA, SH_LB, SH_RA, SH_RB, SH_OA, SH_OB = 24, 25, 26, 27, 28, 29, 30
KINDS = 31


def layer_kernel(
    num_layers, num_chips, heads, head_dim,
    x_hbm, wq, wo, w1, w2, g1, g2, out,
    xg, a_buf, acc, pb, pr, sb, rb, qkv, o_buf, h_buf, st, mb, rsb, w,
    wsem, xsem, ssem, rsem,
):
    seq = xg.shape[1]
    bw = xg.shape[2]
    half = seq // 2
    hw = bw // 2
    model_dim = num_chips * bw
    tp = 2 * num_chips
    me = lax.axis_index("tp")
    chip = me // 2
    core = me % 2
    mine = pl.ds(pl.multiple_of(core * half, half), half)
    theirs = pl.ds(pl.multiple_of((1 - core) * half, half), half)

    def chip_at(r):
        return lax.rem(chip + r, num_chips)

    def block(r):
        return pl.ds(pl.multiple_of(chip_at(r) * bw, bw), bw)

    right = chip_at(1) * 2 + core
    left = chip_at(3) * 2 + core
    partner = chip * 2 + (1 - core)
    half_a = pl.ds(0, hw)
    half_b = pl.ds(hw, hw)

    def copies(l, k):
        s = k % SLOTS
        res = []

        def slab(t, r, col):
            res.append((wq.at[l, t, block(r), :], w.at[s, :, pl.ds(col, head_dim)]))

        if k in (0, 2, 3, 5):
            r = {0: 0, 2: 1, 3: 3, 5: 2}[k]
            for t in range(10):
                slab(t, r, t * head_dim)
        elif k in (1, 4):
            for n, r in enumerate({1: (0, 1), 4: (3, 2)}[k]):
                for t in range(5):
                    slab(10 + t, r, n * hw + t * head_dim)
        elif k < 8:
            for n, r in enumerate({6: (2, 1), 7: (3, 0)}[k]):
                res.append((wo.at[l, :, block(r)], w.at[s, pl.ds(n * hw, hw), :]))
        elif k < 16:
            r = (0, 1, 3, 2)[(k - 8) // 2]
            res.append((w1.at[l, block(r), pl.ds((k % 2) * bw, bw)], w.at[s]))
        else:
            r = (2, 1, 3, 0)[(k - 16) // 2]
            res.append((w2.at[l, pl.ds((k % 2) * bw, bw), block(r)], w.at[s]))
        return [pltpu.make_async_copy(a, b, wsem.at[s]) for a, b in res]

    def load(l, k):
        for c in copies(l, k):
            c.start()

    def load_after(l, k):
        n = k + SLOTS
        if n < LOADS:
            load(l, n)
        else:
            @pl.when(l + 1 < num_layers)
            def _():
                load(l + 1, n - LOADS)

    def wait_w(k):
        s = k % SLOTS
        pltpu.make_async_copy(w.at[s], w.at[s], wsem.at[s]).wait()

    def rc(kind, src, dst, dev):
        return pltpu.make_async_remote_copy(
            src_ref=src, dst_ref=dst, send_sem=ssem.at[kind], recv_sem=rsem.at[kind],
            device_id={"tp": dev}, device_id_type=pl.DeviceIdType.MESH,
        )

    def msg(kind):
        if kind < 4:
            return rc(kind, pb.at[kind, theirs, :], pr.at[kind], partner)
        if kind < STAT:
            n = kind - M1R
            return rc(kind, sb.at[n], rb.at[n], right if n % 2 == 0 else left)
        if kind < STAT + 8:
            d, o = (kind - STAT) // 2, (kind - STAT) % 2
            dev = chip_at(d) * 2 + (core if o == 0 else 1 - core)
            return rc(kind, st.at[0, core], st.at[(4 - d) % 4, core], dev)
        if kind == OWN_RA:
            return rc(kind, xg.at[0, mine, half_a], xg.at[3, mine, half_a], right)
        if kind == OWN_RB:
            return rc(kind, xg.at[0, mine, half_b], xg.at[3, mine, half_b], right)
        if kind == OWN_LA:
            return rc(kind, xg.at[0, mine, half_a], xg.at[1, mine, half_a], left)
        if kind == OWN_LB:
            return rc(kind, xg.at[0, mine, half_b], xg.at[1, mine, half_b], left)
        if kind == FWD_R:
            return rc(kind, xg.at[3, mine, half_a], xg.at[2, mine, half_a], right)
        if kind == FWD_L:
            return rc(kind, xg.at[1, mine, half_b], xg.at[2, mine, half_b], left)
        if kind == SH_OWN:
            return rc(kind, xg.at[0, mine, :], xg.at[0, mine, :], partner)
        r, hf = {SH_LA: (3, half_a), SH_LB: (3, half_b), SH_RA: (1, half_a), SH_RB: (1, half_b),
                 SH_OA: (2, half_a), SH_OB: (2, half_b)}[kind]
        return rc(kind, xg.at[r, mine, hf], xg.at[r, mine, hf], partner)

    def send(*kinds):
        for kind in kinds:
            msg(kind).start()

    def recv(*kinds):
        for kind in kinds:
            msg(kind).wait_recv()

    def block_stats(r, h):
        x = xg[r, pl.ds(pl.multiple_of(h * half, half), half), :].astype(F32)
        mean = jnp.sum(x, axis=1, keepdims=True) * (1.0 / bw)
        d = x - mean
        m2 = jnp.sum(d * d, axis=1, keepdims=True)
        lane = lax.broadcasted_iota(jnp.int32, (half, 128), 1)
        both = jnp.where(lane == 0, mean, m2)
        st[r, h] = both.T[0:8, :]

    def combine_stats():
        for h in range(2):
            means = [st[r, h, 0:1, :] for r in range(num_chips)]
            m2s = [st[r, h, 1:2, :] for r in range(num_chips)]
            mean = sum(means[1:], means[0]) * (1.0 / num_chips)
            dev = [(m - mean) * (m - mean) for m in means]
            m2 = sum(m2s[1:], m2s[0]) + bw * sum(dev[1:], dev[0])
            rstd = lax.rsqrt(m2 * (1.0 / model_dim) + 1e-5)
            rows = pl.ds(h * half, half)
            mb[rows, :] = jnp.broadcast_to(mean, (128, half)).T
            rsb[rows, :] = jnp.broadcast_to(rstd, (128, half)).T

    def normalise(l, r, gain):
        base = chip_at(r) * bw

        def tile(n, c):
            cols = pl.ds(pl.multiple_of(n * 128, 128), 128)
            g = gain[:, pl.ds(pl.multiple_of(base + n * 128, 128), 128)]
            row = lax.broadcasted_iota(jnp.int32, g.shape, 0)
            g = jnp.sum(jnp.where(row == l, g, 0.0), axis=0, keepdims=True)
            x = xg[r, :, cols].astype(F32)
            a_buf[:, cols] = ((x - mb[...]) * rsb[...] * g).astype(BF16)
            return c

        lax.fori_loop(0, bw // 128, tile, 0)

    def cons_qkv(l, pos):
        r = (0, 1, 3, 2)[pos]
        main, extra, ecol = ((0, 1, 0), (2, 1, hw), (3, 4, 0), (5, 4, hw))[pos]
        normalise(l, r, g1)
        wait_w(main)
        if pos in (0, 2):
            wait_w(extra)
        nh = hw // head_dim

        def tile(n, c):
            third = n // 2
            slot = main + third * (extra - main)
            col = pl.multiple_of((n - 2 * third) * hw + third * ecol, hw)
            part = jnp.dot(a_buf[...], w[slot, :, pl.ds(col, hw)], preferred_element_type=F32)
            cols = pl.ds(pl.multiple_of(n * hw, hw), hw)
            if pos > 0:
                part = acc[:, cols] + part
            if pos < 3:
                acc[:, cols] = part
            else:
                for t in range(nh):
                    qkv[n * nh + t] = part[:, t * head_dim:(t + 1) * head_dim].astype(BF16)
            return c

        lax.fori_loop(0, 3, tile, 0)
        load_after(l, main)
        if pos in (1, 3):
            load_after(l, extra)

    def cons_up(l, pos):
        r = (0, 1, 3, 2)[pos]
        k0 = 8 + 2 * pos
        normalise(l, r, g2)
        wait_w(k0)
        wait_w(k0 + 1)

        def tile(n, c):
            slot = k0 % SLOTS + n // 2
            col = pl.multiple_of((n % 2) * hw, hw)
            part = jnp.dot(a_buf[...], w[slot, :, pl.ds(col, hw)], preferred_element_type=F32)
            cols = pl.ds(pl.multiple_of(n * hw, hw), hw)
            if pos > 0:
                part = acc[:, cols] + part
            if pos < 3:
                acc[:, cols] = part
            else:
                h_buf[:, cols] = jax.nn.gelu(part, approximate=True).astype(BF16)
            return c

        lax.fori_loop(0, 4, tile, 0)
        load_after(l, k0)
        load_after(l, k0 + 1)

    def prod_out(l, d):
        k = 6 if d in (2, 1) else 7
        row = 0 if d in (2, 3) else hw
        if row == 0:
            wait_w(k)

        def tile(n, c):
            cols = pl.ds(pl.multiple_of(n * hw, hw), hw)
            pb[d, :, cols] = jnp.dot(
                o_buf[...], w[k % SLOTS, pl.ds(row, hw), cols], preferred_element_type=F32).astype(BF16)
            return c

        lax.fori_loop(0, 2, tile, 0)
        if row:
            load_after(l, k)

    def prod_down(l, d):
        k0 = {2: 16, 1: 18, 3: 20, 0: 22}[d]
        s0 = k0 % SLOTS
        wait_w(k0)
        wait_w(k0 + 1)

        def tile(n, c):
            cols = pl.ds(pl.multiple_of(n * hw, hw), hw)
            part = jnp.dot(h_buf[:, 0:bw], w[s0, :, cols], preferred_element_type=F32)
            part += jnp.dot(h_buf[:, bw:2 * bw], w[s0 + 1, :, cols], preferred_element_type=F32)
            pb[d, :, cols] = part.astype(BF16)
            return c

        lax.fori_loop(0, 2, tile, 0)
        load_after(l, k0)
        load_after(l, k0 + 1)

    def pair_sum(d, cols):
        return pb[d, mine, cols].astype(F32) + pr[d, :, cols].astype(F32)

    def reduce_scatter(prod):
        prod(2)
        send(PAIR + 2)
        prod(1)
        send(PAIR + 1)
        recv(PAIR + 2)
        sb[0] = pair_sum(2, half_a).astype(BF16)
        sb[1] = pair_sum(2, half_b).astype(BF16)
        send(M1R, M1L)
        prod(3)
        send(PAIR + 3)
        recv(PAIR + 1)
        sb[2] = pair_sum(1, half_b).astype(BF16)
        send(M2R)
        prod(0)
        send(PAIR + 0)
        recv(PAIR + 3)
        sb[3] = pair_sum(3, half_a).astype(BF16)
        send(M2L)
        recv(M1R)
        sb[4] = (pair_sum(1, half_a) + rb[0].astype(F32)).astype(BF16)
        send(M3R)
        recv(M1L)
        sb[5] = (pair_sum(3, half_b) + rb[1].astype(F32)).astype(BF16)
        send(M3L)
        recv(PAIR + 0, M2L, M3R)
        xg[0, mine, half_a] = (xg[0, mine, half_a].astype(F32) + (
            pair_sum(0, half_a) + rb[3].astype(F32) + rb[4].astype(F32))).astype(BF16)
        recv(M2R, M3L)
        xg[0, mine, half_b] = (xg[0, mine, half_b].astype(F32) + (
            pair_sum(0, half_b) + rb[2].astype(F32) + rb[5].astype(F32))).astype(BF16)

    def gather(cons):
        stats = [STAT + n for n in range(1, 8)]
        block_stats(0, core)
        send(*stats)
        send(OWN_RA, OWN_LB, OWN_RB, OWN_LA, SH_OWN)
        recv(*stats)
        combine_stats()
        recv(SH_OWN)
        cons(0)
        recv(OWN_RA)
        send(FWD_R, SH_LA)
        recv(OWN_LB)
        send(FWD_L, SH_RB)
        recv(OWN_RB)
        send(SH_LB)
        recv(OWN_LA)
        send(SH_RA)
        recv(SH_RA, SH_RB)
        cons(1)
        recv(SH_LA, SH_LB)
        cons(2)
        recv(FWD_R)
        send(SH_OA)
        recv(FWD_L)
        send(SH_OB)
        recv(SH_OA, SH_OB)
        cons(3)
        for kind in range(KINDS):
            if kind != STAT:
                msg(kind).wait_send()

    def attention():
        scale = 1.0 / math.sqrt(head_dim)
        q_pos = lax.broadcasted_iota(jnp.int32, (seq, seq), 0)
        k_pos = lax.broadcasted_iota(jnp.int32, (seq, seq), 1)
        keep = k_pos <= q_pos
        for h in range(heads):
            s = lax.dot_general(qkv[3 * h], qkv[3 * h + 1], (((1,), (1,)), ((), ())),
                                preferred_element_type=F32) * scale
            s = jnp.where(keep, s, -1e30)
            p = jnp.exp(s - jnp.max(s, axis=1, keepdims=True))
            total = jnp.sum(p, axis=1, keepdims=True)
            mix = jnp.dot(p.astype(BF16), qkv[3 * h + 2], preferred_element_type=F32)
            o_buf[:, h * head_dim:(h + 1) * head_dim] = (mix / total).astype(BF16)

    x_copies = [pltpu.make_async_copy(x_hbm.at[:, block(r)], xg.at[r], xsem.at[r]) for r in range(num_chips)]
    for c in x_copies:
        c.start()
    for k in range(SLOTS):
        load(0, k)

    barrier = pltpu.get_barrier_semaphore()
    for n in range(1, tp):
        pl.semaphore_signal(barrier, inc=1, device_id={"tp": lax.rem(me + n, tp)},
                            device_id_type=pl.DeviceIdType.MESH)
    for c in x_copies:
        c.wait()

    def first_stats(n, c):
        block_stats(n // 2, n % 2)
        return c

    lax.fori_loop(0, 2 * num_chips, first_stats, 0)
    combine_stats()
    for pos in range(4):
        cons_qkv(0, pos)
    pl.semaphore_wait(barrier, tp - 1)

    def layer(l, c):
        attention()
        reduce_scatter(functools.partial(prod_out, l))
        gather(functools.partial(cons_up, l))
        reduce_scatter(functools.partial(prod_down, l))

        def next_qkv(pos):
            @pl.when(l + 1 < num_layers)
            def _():
                cons_qkv(l + 1, pos)

        gather(next_qkv)
        return c

    lax.fori_loop(0, num_layers, layer, 0)
    outs = [pltpu.make_async_copy(xg.at[r], out.at[:, block(r)], xsem.at[r]) for r in range(num_chips)]
    for c in outs:
        c.start()
    for c in outs:
        c.wait()


def solution(mesh):
    tp = mesh.shape["tp"]
    num_chips = tp // 2

    def device_fn(act_in, w_qkv, w_out, w_up, w_down, gain_one, gain_two):
        seq, model_dim = act_in.shape
        num_layers, _, heads, _, head_dim = w_qkv.shape
        ffn = w_up.shape[2]
        bw = model_dim // num_chips
        half, hw = seq // 2, bw // 2
        wq = jnp.transpose(w_qkv, (0, 2, 3, 1, 4)).reshape(num_layers, heads * 3, model_dim, head_dim)
        wo = w_out.reshape(num_layers, heads * head_dim, model_dim)
        vmem = pl.BlockSpec(memory_space=pltpu.VMEM)
        hbm = pl.BlockSpec(memory_space=pl.ANY)
        return pl.pallas_call(
            functools.partial(layer_kernel, num_layers, num_chips, heads, head_dim),
            out_shape=jax.ShapeDtypeStruct((seq, model_dim), BF16),
            in_specs=[hbm] * 5 + [vmem] * 2,
            out_specs=hbm,
            scratch_shapes=[
                pltpu.VMEM((num_chips, seq, bw), BF16),
                pltpu.VMEM((seq, bw), BF16),
                pltpu.VMEM((seq, ffn), F32),
                pltpu.VMEM((num_chips, seq, bw), BF16),
                pltpu.VMEM((num_chips, half, bw), BF16),
                pltpu.VMEM((6, half, hw), BF16),
                pltpu.VMEM((6, half, hw), BF16),
                pltpu.VMEM((heads * 3, seq, head_dim), BF16),
                pltpu.VMEM((seq, heads * head_dim), BF16),
                pltpu.VMEM((seq, ffn), BF16),
                pltpu.VMEM((num_chips, 2, 8, 128), F32),
                pltpu.VMEM((seq, 128), F32),
                pltpu.VMEM((seq, 128), F32),
                pltpu.VMEM((SLOTS, bw, bw), BF16),
                pltpu.SemaphoreType.DMA((SLOTS,)),
                pltpu.SemaphoreType.DMA((num_chips,)),
                pltpu.SemaphoreType.DMA((KINDS,)),
                pltpu.SemaphoreType.DMA((KINDS,)),
            ],
            compiler_params=pltpu.CompilerParams(
                collective_id=0, has_side_effects=True, vmem_limit_bytes=60 * 2 ** 20),
            name="layers",
        )(act_in, wq, wo, w_up, w_down, gain_one, gain_two)

    return jax.shard_map(
        device_fn,
        mesh=mesh,
        in_specs=(
            P("dp", None),
            P(None, None, "tp", None, None),
            P(None, "tp", None, None),
            P(None, None, "tp"),
            P(None, "tp", None),
            P(None, None),
            P(None, None),
        ),
        out_specs=P("dp", None),
        check_vma=False,
    )
```

time: 364 us -> 182 us (0.50)
  waiting for transfers between devices: 236 us -> 0 us
  Pallas kernels: 0 us -> 178 us
  matrix products: 86.8 us -> 0 us
  other arithmetic: 19.4 us -> 0 us
  between operations: 13.3 us -> 0.01 us
    psum x4 -> x0, waiting for transfers between devices: 235 us -> none  [the longest x2 118 us: device_fn(): attn_sum = lax.psum(part_sum, 'tp')]
    pallas_call x0 -> x1, Pallas kernels: none -> 178 us  [device_fn(): pl.pallas_call(functools.partial(layer_kernel, num_layers, num_chips, hea...]
    dot_general x8 -> x0, matrix products: 86.8 us -> none  [the longest x2 48.7 us: device_fn(): jnp.dot(hidden, w_down[layer_idx], preferred_element_type=jnp.float32)]
    reduce_sum x10 -> x0, other arithmetic: 15.1 us -> none  [the longest x4 11.4 us: layer_norm(): centred = rows_f32 - jnp.mean(rows_f32, axis=-1, keepdims=True)]
    convert_element_type x1 -> x0, other arithmetic: 4.2 us -> none  [device_fn(): (act_rows.astype(jnp.float32) + mlp_sum.astype(jnp.float32)).astype(jnp.b...]
  transfers between devices with their start and end apart: 4 -> 0, of which waited for: 4 -> 0; matrix products, arithmetic and copies ran while one was open for 0% -> 0% of each run, Pallas kernels for 0% -> 0%
where the time goes in v1:
time: 182 us; the launch traced here: 181 us
  Pallas kernels  178 us (98%)
  local copies, waits for them, and re-layouts  3.4 us (2%)
    pallas_call x1, Pallas kernels, device_fn(): pl.pallas_call(functools.partial(layer_kernel, num_layers, num_chips, hea...  178 us

profile of v1, /device:TPU:113, one launch (start us, length us, event | category | flops | bytes accessed | tf_op | source)
XLA Modules:
  0.0 181.5 jit_solution(2061144783889292021)
XLA Ops:
  0.0 178.1 %layers.1 = bf16[256,5120]{1,0:T(8,128)(2,1)} custom-call(bf16[256,5120]{1,0:T(8,128)(2,1)} %x_hbm.1, bf16[2,15,5120,128]{3,2,1,0:T(8,128)(2,1)} %bitcast.4, bf16[2,640,5120]{2,1,0:T(8,128)(2,1)} %bitcast.5, bf16[2,5120,2560]{2,1,0:T(8,128)(2,1)} %w1.1, bf16[2,2560,5120]{2,1,0:T(8,128)(2,1)} %w2.1, f32[2,5120]{1,0:T(2,128)} %g1.1, f32[2,5120]{1,0:T(2,128)} %g2.1), custom_call_target="tpu_custom_call" | custom-call | tf_op jit(solution)/shard_map/layers/pallas_call | solution.py:397
  178.1 3.4 %copy.9 = bf16[256,5120]{1,0:T(8,128)(2,1)} copy(bf16[256,5120]{1,0:T(8,128)(2,1)} %layers.1) | data formatting | bytes 5242880
